TPU v7x, 32 devices: a whole 2x2x4 slice. The times are simulated.
32 devices in a mesh: blk: 8 (over y, x, core), grp: 4 (over z).
Axes of the slice: x: 2, y: 2, z: 4, core: 2. Of those that a mesh axis runs over, the one named last changes fastest.
Arguments:
- samples: float32 [32, 128, 256], P('blk', 'grp'), may hold values from -11 to 11
- pair_table: int32 [32, 16], P('blk'), may hold values from 0 to 31
- assignment: int32 [2, 32], P(None, 'blk'), may hold values from 0 to 127
- band_index: int32 [2], replicated, may hold values from 0 to 1023
Outputs:
- log_weight: float32 [2, 32, 128], P(None, 'blk', 'grp')
All inputs are finite; a program needn't handle non-finite values.
Results may differ from a plain program's by a relative error of at most 0.0003.
Values sent between devices are 32-bit elements; how exact they have to be, the bound alone decides.
No kernel may reach another device: no remote copies, remote signals or barrier semaphores. Data moves between devices by JAX's collectives and lax.ppermute only.
A program may use at most 128 MiB of HBM per device.

v0:
```python
import jax
import jax.numpy as jnp
from jax import lax
from jax.sharding import PartitionSpec as P

PAIRS = 16


def joined_2(shard, axis, combine):
    everything = jax.tree.map(lambda part: lax.all_gather(part, axis), shard)
    initial = jax.tree.map(lambda part: part[0], everything)

    def hop(k, so_far):
        return combine(so_far, jax.tree.map(lambda part: part[k], everything))

    return lax.fori_loop(1, lax.axis_size(axis), hop, initial)


def make_fold(queries, query_norm, band_list, counts):

    def fold(state, shard_rows, offset):
        count_in = shard_rows.shape[0]
        rows_dev = shard_rows.shape[1]

        def compute(inner):
            key_rows = shard_rows.reshape(count_in * rows_dev, shard_rows.shape[2])
            key_norm = jnp.sum(key_rows * key_rows, -1)
            product = jnp.einsum("qd,kd->qk", queries, key_rows, precision=lax.Precision.HIGHEST)
            distance = query_norm[:, None] + key_norm[None, :] - 2.0 * product
            blocks = []
            for band_sq in band_list:
                scores = (-distance / (2.0 * band_sq)).reshape(
                    distance.shape[0], count_in, rows_dev
                )
                peak = jnp.max(scores, -1)
                blocks.append(peak + jnp.log(jnp.sum(jnp.exp(scores - peak[..., None]), -1)))
            update = jnp.stack(blocks)
            return lax.dynamic_update_slice(inner, update, (0, 0, offset))

        needed = jnp.any(counts > 0)
        return lax.cond(needed, compute, lambda inner: inner, state)

    return fold


def per_device(samples, pair_table, assignment, band_index):
    local_subs, rows_dev, width = samples.shape
    rounds = assignment.shape[0]
    group_size = lax.axis_size("grp")
    group_index = lax.axis_index("grp")
    members = local_subs * lax.axis_size("blk")
    band_sq = width * (1.0 + band_index.astype(jnp.float32) / 256.0) / 32.0
    local_pick = assignment - group_index * rows_dev
    onehot = (
        local_pick[:, :, None] == jnp.arange(rows_dev, dtype=jnp.int32)[None, None, :]
    ).astype(jnp.float32)
    picked = jnp.einsum("tsr,srd->td", onehot, samples, precision=lax.Precision.HIGHEST)
    centre = lax.psum(picked, ("blk", "grp")) / members
    member_ids = jnp.arange(members, dtype=jnp.int32)
    count_int = jnp.sum(
        (pair_table[:, :, None] == member_ids[None, None, :]).astype(jnp.int32), axis=1
    )
    counts = count_int.astype(jnp.float32)
    gathered = lax.all_gather(samples, "grp", axis=1, tiled=True)
    query_count = local_subs * rows_dev * group_size
    queries = gathered.reshape(query_count, width)
    query_norm = jnp.sum(queries * queries, -1)
    start_state = jnp.zeros((rounds, query_count, members), jnp.float32)
    fold = make_fold(queries, query_norm, [band_sq[turn] for turn in range(rounds)], count_int)
    partial_value = fold(
        start_state, lax.all_gather(samples, "blk", axis=0, tiled=True), jnp.int32(0)
    )
    split_view = partial_value.reshape(rounds, local_subs, group_size, rows_dev, members)
    swapped = lax.all_to_all(split_view, "grp", split_axis=2, concat_axis=2, tiled=True)
    peak = jnp.max(swapped, 2)
    kernel = peak + jnp.log(jnp.sum(jnp.exp(swapped - peak[:, :, None]), 2))
    weighted = jnp.einsum("tsrm,sm->tsr", kernel, counts, precision=lax.Precision.HIGHEST) / PAIRS
    spread = samples[None] - centre[:, None, None, :]
    logits = weighted - jnp.sum(spread * spread, -1) / (2.0 * band_sq[:, None, None])
    row_peak = jnp.max(logits, -1)
    row_total = jnp.sum(jnp.exp(logits - row_peak[..., None]), -1)

    def combine_pair(first, second):
        joined = jnp.maximum(first[0], second[0])
        return (
            joined,
            first[1] * jnp.exp(first[0] - joined) + second[1] * jnp.exp(second[0] - joined),
        )

    peak_all, total_all = joined_2((row_peak, row_total), "grp", combine_pair)
    return logits - peak_all[..., None] - jnp.log(total_all)[..., None]


def solution(mesh):
    return jax.shard_map(
        per_device,
        mesh=mesh,
        in_specs=(P("blk", "grp", None), P("blk", None), P(None, "blk"), P()),
        out_specs=P(None, "blk", "grp"),
        check_vma=False,
    )
```

profile of v0, /device:TPU:0, one launch (start us, length us, event | category | flops | bytes accessed | tf_op | source)
XLA Modules:
  0.0 123.1 jit_solution(9642932200936565193)
XLA Ops:
  6.5 0.7 all-gather.6.cloned.1.call-update
  7.3 0.8 convert_reduce_fusion
  8.0 0.6 compare_reduce_fusion
  9.3 0.7 broadcast_subtract_fusion
  10.1 1.2 convolution_bitcast_fusion
  11.3 42.0 %psum.7 = f32[2,256]{1,0:T(2,128)S(1)} all-reduce(f32[2,256]{1,0:T(2,128)S(1)} %convolution_bitcast_fusion), channel_id=1, replica_groups=mesh['blk'=8,'grp'=4] {'blk','grp'}, use_global_device_ids=true, to_apply=%region_12.0 | all-reduce | flops 512 | bytes 4096 | tf_op jit(solution)/shard_map/psum | solution.py:58
  53.2 15.9 %all_gather.18 = f32[4,128,256]{2,1,0:T(8,128)S(1)} all-gather(f32[4,32,256]{2,1,0:T(8,128)} %param.8), channel_id=1, replica_groups=mesh['blk'=8,'grp'=4] {'grp'}, dimensions={1}, use_global_device_ids=true | all-gather | bytes 655360 | tf_op jit(solution)/shard_map/all_gather | solution.py:64
  69.2 0.7 multiply_add_fusion
  69.8 14.7 %conditional.1 = (f32[2,512,32]{1,2,0:T(8,128)S(1)}) conditional(s32[]{:T(128)} %convert_element_type.15, () %tuple.36, (f32[4,128,256]{2,1,0:T(8,128)S(1)}, f32[32,32,256]{2,1,0:T(8,128)}, f32[2]{0:T(128)S(1)}) %tuple.37), branch_computations={%region_2.0_spmd, %region_3.10_spmd} | conditional | flops 1617689088 | bytes 25186376 | solution.py:41
  69.8 1.4 %multiply_reduce_fusion = f32[32,32]{1,0:T(8,128)S(1)} fusion(f32[32,32,256]{2,1,0:T(8,128)} %get-tuple-element.164), kind=kLoop, calls=%fused_computation.11 | loop fusion | flops 523264 | bytes 1052672 | tf_op jit(solution)/shard_map/cond/branch_1_fun/reduce_sum | solution.py:27
  71.3 0.7 fusion.12
  73.5 5.3 %broadcast_divide_fusion.1 = (f32[512,1024]{1,0:T(8,128)}, f32[512,1024]{1,0:T(8,128)}) fusion(f32[]{:T(128)} %bitcast.3, f32[]{:T(128)} %bitcast.6, f32[512,256]{1,0:T(8,128)S(1)} %bitcast.71, f32[1024,256]{1,0:T(8,128)} %bitcast.74, f32[1024]{0:T(1024)S(1)} %add.87, f32[512]{0:T(512)S(1)} %bitcast.80), kind=kOutput, calls=%fused_computation.10 | convolution fusion | flops 1613758464 | bytes 5773320 | tf_op jit(solution)/shard_map/cond/branch_1_fun/qd,kd->qk/dot_general | solution.py:28
  78.8 1.9 %copy.16 = f32[512,1024]{0,1:T(8,128)S(1)} copy(f32[512,1024]{1,0:T(8,128)} %get-tuple-element.190) | data formatting | bytes 4194304 | tf_op jit(solution)/shard_map/cond/branch_1_fun/div | solution.py:32
  81.1 0.5 fusion.3
  81.6 1.9 %copy.17 = f32[512,1024]{0,1:T(8,128)S(1)} copy(f32[512,1024]{1,0:T(8,128)} %get-tuple-element.191) | data formatting | bytes 4194304 | tf_op jit(solution)/shard_map/cond/branch_1_fun/div | solution.py:32
  83.9 0.5 fusion.1
  84.9 1.0 reshape.97
  85.9 3.8 %all-to-all-start = ((f32[4,1,8192]{2,1,0:T(1,128)}), f32[4,1,8192]{2,1,0:T(1,128)S(1)}, u32[]{:S(2)}, u32[]{:S(2)}) async-start(f32[4,1,8192]{2,1,0:T(1,128)} %reshape.97), calls=%async_computation | async-start | bytes 262144 | tf_op jit(solution)/shard_map/all_to_all | solution.py:74
  89.8 5.8 %all-to-all-done = f32[4,1,8192]{2,1,0:T(1,128)S(1)} async-done(((f32[4,1,8192]{2,1,0:T(1,128)}), f32[4,1,8192]{2,1,0:T(1,128)S(1)}, u32[]{:S(2)}, u32[]{:S(2)}) %all-to-all-start) | async-done | bytes 131104 | tf_op jit(solution)/shard_map/all_to_all | solution.py:74
  95.6 0.5 broadcast.44
  96.1 1.0 reduce.5
  98.3 9.0 %all-gather.3 = f32[4,2,4]{2,1,0:T(2,128)S(1)} all-gather(f32[1,2,4]{2,1,0:T(2,128)S(1)} %bitcast.79), channel_id=3, replica_groups=mesh['blk'=8,'grp'=4] {'grp'}, dimensions={0}, use_global_device_ids=true | all-gather | bytes 160 | tf_op jit(solution)/shard_map/all_gather | solution.py:10
  107.3 8.2 %all-gather.2 = f32[4,2,4]{2,1,0:T(2,128)S(1)} all-gather(f32[1,2,4]{2,1,0:T(2,128)S(1)} %bitcast.77), channel_id=2, replica_groups=mesh['blk'=8,'grp'=4] {'grp'}, dimensions={0}, use_global_device_ids=true | all-gather | bytes 160 | tf_op jit(solution)/shard_map/all_gather | solution.py:10
  115.6 0.7 subtract_subtract_fusion
  (31 shorter events, 2.9 us)
Async XLA Ops:
  6.5 63.3 %all-gather.6.cloned.1.call-start = ((), (), s32[]{:S(2)}) async-start(), calls=%async_computation.1 | async-start | bytes 1179648 | tf_op jit(solution)/shard_map/all_gather | solution.py:71
  84.5 5.2 %copy-start = (f32[4,32,256]{2,1,0:T(8,128)S(1)}, f32[4,32,256]{2,1,0:T(8,128)}, u32[]{:S(2)}) copy-start(f32[4,32,256]{2,1,0:T(8,128)} %param.8) | copy-start | bytes 393220
  85.9 9.7 %all-to-all-start = ((f32[4,1,8192]{2,1,0:T(1,128)}), f32[4,1,8192]{2,1,0:T(1,128)S(1)}, u32[]{:S(2)}, u32[]{:S(2)}) async-start(f32[4,1,8192]{2,1,0:T(1,128)} %reshape.97), calls=%async_computation | async-start | bytes 262144 | tf_op jit(solution)/shard_map/all_to_all | solution.py:74
Sparse Core Ops, SparseCore 0:
  9.2 26.2 all-gather.5
where the time goes:
time: 124 us; the launch traced here: 123 us
  blocking collectives  75 us (60%)
  between operations  14.1 us (11%)
  other arithmetic  8.66 us (7%)
  local copies, waits for them, and re-layouts  6.86 us (6%)
  matrix products  6.7 us (5%)
  waiting for transfers between devices  6.5 us (5%)
  starting transfers between devices  3.8 us (3%)
  loops' own time  1.43 us (1%)
    psum x1, blocking collectives, per_device(): centre = lax.psum(picked, ('blk', 'grp')) / members  42 us
    all_gather x2, blocking collectives, joined_2(): everything = jax.tree.map(lambda part: lax.all_gather(part, axis), shard)  17.2 us
    all_gather x1, blocking collectives, per_device(): gathered = lax.all_gather(samples, 'grp', axis=1, tiled=True)  15.9 us
    all_to_all x1, waiting for transfers between devices, per_device(): lax.all_to_all(split_view, 'grp', split_axis=2, concat_axis=2, tiled=True)  5.79 us
    dot_general x1, matrix products, compute(): jnp.einsum('qd,kd->qk', queries, key_rows, precision=lax.Precision.HIGHEST)  5.35 us
    div x2, local copies, waits for them, and re-layouts, compute(): -distance / (2.0 * band_sq)  3.84 us
    all_to_all x1, starting transfers between devices, per_device(): lax.all_to_all(split_view, 'grp', split_axis=2, concat_axis=2, tiled=True)  3.8 us
  transfers between devices with their start and end apart: 2, of which 1 were waited for; matrix products, arithmetic and copies ran while one was open for 3% of the time, Pallas kernels for 0%

commit v1 on v0

--- a/solution.py
+++ b/solution.py
@@ -55,7 +55,7 @@
         local_pick[:, :, None] == jnp.arange(rows_dev, dtype=jnp.int32)[None, None, :]
     ).astype(jnp.float32)
     picked = jnp.einsum("tsr,srd->td", onehot, samples, precision=lax.Precision.HIGHEST)
-    centre = lax.psum(picked, ("blk", "grp")) / members
+    centre = lax.psum(lax.psum(picked, axis_name="grp"), axis_name="blk") / members
     member_ids = jnp.arange(members, dtype=jnp.int32)
     count_int = jnp.sum(
         (pair_table[:, :, None] == member_ids[None, None, :]).astype(jnp.int32), axis=1

time: 124 us -> 107 us (0.86)
  blocking collectives: 75 us -> 58.9 us
    psum x1 -> x2, blocking collectives: 42 us -> 25.4 us  [the longest x1 13.5 us: per_device(): lax.psum(picked, axis_name='grp')]
  transfers between devices with their start and end apart: 2 -> 2, of which waited for: 1 -> 1; matrix products, arithmetic and copies ran while one was open for 3% -> 4% of each run, Pallas kernels for 0% -> 0%
where the time goes in v1:
time: 107 us; the launch traced here: 106 us
  blocking collectives  58.9 us (55%)
  between operations  14.2 us (13%)
  other arithmetic  8.66 us (8%)
  local copies, waits for them, and re-layouts  6.86 us (6%)
  matrix products  6.7 us (6%)
  waiting for transfers between devices  6.45 us (6%)
  starting transfers between devices  3.32 us (3%)
  loops' own time  1.43 us (1%)
    all_gather x2, blocking collectives, joined_2(): everything = jax.tree.map(lambda part: lax.all_gather(part, axis), shard)  17.2 us
    all_gather x1, blocking collectives, per_device(): gathered = lax.all_gather(samples, 'grp', axis=1, tiled=True)  16.3 us
    psum x1, blocking collectives, per_device(): lax.psum(picked, axis_name='grp')  13.5 us
    psum x1, blocking collectives, per_device(): lax.psum(lax.psum(picked, axis_name='grp'), axis_name='blk') / members  11.9 us
    all_to_all x1, waiting for transfers between devices, per_device(): lax.all_to_all(split_view, 'grp', split_axis=2, concat_axis=2, tiled=True)  5.73 us
    dot_general x1, matrix products, compute(): jnp.einsum('qd,kd->qk', queries, key_rows, precision=lax.Precision.HIGHEST)  5.35 us
    div x2, local copies, waits for them, and re-layouts, compute(): -distance / (2.0 * band_sq)  3.84 us
    all_to_all x1, starting transfers between devices, per_device(): lax.all_to_all(split_view, 'grp', split_axis=2, concat_axis=2, tiled=True)  3.32 us
  transfers between devices with their start and end apart: 2, of which 1 were waited for; matrix products, arithmetic and copies ran while one was open for 4% of the time, Pallas kernels for 0%

profile of v1, /device:TPU:0, one launch (start us, length us, event | category | flops | bytes accessed | tf_op | source)
XLA Modules:
  0.0 106.5 jit_solution(3748019330601630338)
XLA Ops:
  6.5 0.7 all-gather.6.cloned.1.call-update
  7.3 0.8 convert_reduce_fusion
  8.0 0.6 compare_reduce_fusion
  9.3 0.7 broadcast_subtract_fusion
  10.1 1.2 %convolution_bitcast_fusion = f32[2,256]{1,0:T(2,128)S(1)} fusion(f32[4,32,256]{2,1,0:T(8,128)} %param.8, s32[2,4]{0,1:T(4,128)S(1)} %copy.19), kind=kOutput, calls=%fused_computation.22 | convolution fusion | flops 786688 | bytes 133152 | tf_op jit(solution)/shard_map/tsr,srd->td/dot_general | solution.py:57
  11.3 13.5 %psum.14 = f32[2,256]{1,0:T(2,128)S(1)} all-reduce(f32[2,256]{1,0:T(2,128)S(1)} %convolution_bitcast_fusion), channel_id=1, replica_groups=mesh['blk'=8,'grp'=4] {'grp'}, use_global_device_ids=true, to_apply=%region_12.0 | all-reduce | flops 512 | bytes 4096 | tf_op jit(solution)/shard_map/psum | solution.py:58
  24.7 11.9 %psum.15 = f32[2,256]{1,0:T(2,128)S(1)} all-reduce(f32[2,256]{1,0:T(2,128)S(1)} %psum.14), channel_id=1, replica_groups=mesh['blk'=8,'grp'=4] {'blk'}, use_global_device_ids=true, to_apply=%region_13.0 | all-reduce | flops 512 | bytes 4096 | tf_op jit(solution)/shard_map/psum | solution.py:58
  36.7 16.3 %all_gather.18 = f32[4,128,256]{2,1,0:T(8,128)S(1)} all-gather(f32[4,32,256]{2,1,0:T(8,128)} %param.8), channel_id=1, replica_groups=mesh['blk'=8,'grp'=4] {'grp'}, dimensions={1}, use_global_device_ids=true | all-gather | bytes 655360 | tf_op jit(solution)/shard_map/all_gather | solution.py:64
  53.0 0.7 multiply_add_fusion
  53.7 14.7 %conditional.1 = (f32[2,512,32]{1,2,0:T(8,128)S(1)}) conditional(s32[]{:T(128)} %convert_element_type.15, () %tuple.36, (f32[4,128,256]{2,1,0:T(8,128)S(1)}, f32[32,32,256]{2,1,0:T(8,128)}, f32[2]{0:T(128)S(1)}) %tuple.37), branch_computations={%region_2.0_spmd, %region_3.10_spmd} | conditional | flops 1617689088 | bytes 25186376 | solution.py:41
  53.7 1.4 %multiply_reduce_fusion = f32[32,32]{1,0:T(8,128)S(1)} fusion(f32[32,32,256]{2,1,0:T(8,128)} %get-tuple-element.164), kind=kLoop, calls=%fused_computation.11 | loop fusion | flops 523264 | bytes 1052672 | tf_op jit(solution)/shard_map/cond/branch_1_fun/reduce_sum | solution.py:27
  55.2 0.7 fusion.12
  57.4 5.3 %broadcast_divide_fusion.1 = (f32[512,1024]{1,0:T(8,128)}, f32[512,1024]{1,0:T(8,128)}) fusion(f32[]{:T(128)} %bitcast.3, f32[]{:T(128)} %bitcast.6, f32[512,256]{1,0:T(8,128)S(1)} %bitcast.71, f32[1024,256]{1,0:T(8,128)} %bitcast.74, f32[1024]{0:T(1024)S(1)} %add.89, f32[512]{0:T(512)S(1)} %bitcast.80), kind=kOutput, calls=%fused_computation.10 | convolution fusion | flops 1613758464 | bytes 5773320 | tf_op jit(solution)/shard_map/cond/branch_1_fun/qd,kd->qk/dot_general | solution.py:28
  62.7 1.9 %copy.16 = f32[512,1024]{0,1:T(8,128)S(1)} copy(f32[512,1024]{1,0:T(8,128)} %get-tuple-element.190) | data formatting | bytes 4194304 | tf_op jit(solution)/shard_map/cond/branch_1_fun/div | solution.py:32
  65.5 1.9 %copy.17 = f32[512,1024]{0,1:T(8,128)S(1)} copy(f32[512,1024]{1,0:T(8,128)} %get-tuple-element.191) | data formatting | bytes 4194304 | tf_op jit(solution)/shard_map/cond/branch_1_fun/div | solution.py:32
  67.8 0.5 fusion.1
  68.8 1.0 reshape.97
  69.8 3.3 %all-to-all-start = ((f32[4,1,8192]{2,1,0:T(1,128)}), f32[4,1,8192]{2,1,0:T(1,128)S(1)}, u32[]{:S(2)}, u32[]{:S(2)}) async-start(f32[4,1,8192]{2,1,0:T(1,128)} %reshape.97), calls=%async_computation | async-start | bytes 262144 | tf_op jit(solution)/shard_map/all_to_all | solution.py:74
  73.2 5.7 %all-to-all-done = f32[4,1,8192]{2,1,0:T(1,128)S(1)} async-done(((f32[4,1,8192]{2,1,0:T(1,128)}), f32[4,1,8192]{2,1,0:T(1,128)S(1)}, u32[]{:S(2)}, u32[]{:S(2)}) %all-to-all-start) | async-done | bytes 131104 | tf_op jit(solution)/shard_map/all_to_all | solution.py:74
  79.0 0.5 broadcast.44
  79.5 1.0 reduce.5
  81.7 9.0 %all-gather.3 = f32[4,2,4]{2,1,0:T(2,128)S(1)} all-gather(f32[1,2,4]{2,1,0:T(2,128)S(1)} %bitcast.79), channel_id=3, replica_groups=mesh['blk'=8,'grp'=4] {'grp'}, dimensions={0}, use_global_device_ids=true | all-gather | bytes 160 | tf_op jit(solution)/shard_map/all_gather | solution.py:10
  90.7 8.2 %all-gather.2 = f32[4,2,4]{2,1,0:T(2,128)S(1)} all-gather(f32[1,2,4]{2,1,0:T(2,128)S(1)} %bitcast.77), channel_id=2, replica_groups=mesh['blk'=8,'grp'=4] {'grp'}, dimensions={0}, use_global_device_ids=true | all-gather | bytes 160 | tf_op jit(solution)/shard_map/all_gather | solution.py:10
  99.0 0.7 subtract_subtract_fusion
  (32 shorter events, 3.5 us)
Async XLA Ops:
  6.5 47.1 %all-gather.6.cloned.1.call-start = ((), (), s32[]{:S(2)}) async-start(), calls=%async_computation.1 | async-start | bytes 1179648 | tf_op jit(solution)/shard_map/all_gather | solution.py:71
  68.4 4.8 %copy-start = (f32[4,32,256]{2,1,0:T(8,128)S(1)}, f32[4,32,256]{2,1,0:T(8,128)}, u32[]{:S(2)}) copy-start(f32[4,32,256]{2,1,0:T(8,128)} %param.8) | copy-start | bytes 393220
  69.8 9.2 %all-to-all-start = ((f32[4,1,8192]{2,1,0:T(1,128)}), f32[4,1,8192]{2,1,0:T(1,128)S(1)}, u32[]{:S(2)}, u32[]{:S(2)}) async-start(f32[4,1,8192]{2,1,0:T(1,128)} %reshape.97), calls=%async_computation | async-start | bytes 262144 | tf_op jit(solution)/shard_map/all_to_all | solution.py:74
Sparse Core Ops, SparseCore 0:
  9.2 26.1 all-gather.5

commit v2 on v0

--- a/solution.py
+++ b/solution.py
@@ -4,6 +4,11 @@
 from jax.sharding import PartitionSpec as P
 
 PAIRS = 16
+
+
+def summed_here(x, axis):
+    parts = lax.all_gather(x, axis)
+    return jnp.sum(parts, axis=0)
 
 
 def joined_2(shard, axis, combine):
@@ -55,7 +60,7 @@
         local_pick[:, :, None] == jnp.arange(rows_dev, dtype=jnp.int32)[None, None, :]
     ).astype(jnp.float32)
     picked = jnp.einsum("tsr,srd->td", onehot, samples, precision=lax.Precision.HIGHEST)
-    centre = lax.psum(picked, ("blk", "grp")) / members
+    centre = summed_here(picked, ("blk", "grp")) / members
     member_ids = jnp.arange(members, dtype=jnp.int32)
     count_int = jnp.sum(
         (pair_table[:, :, None] == member_ids[None, None, :]).astype(jnp.int32), axis=1

time: 124 us -> 152 us (1.23)
  blocking collectives: 75 us -> 104 us
    all_gather x0 -> x1, blocking collectives: none -> 70.3 us  [summed_here(): parts = lax.all_gather(x, axis)]
    psum x1 -> x0, blocking collectives: 42 us -> none  [per_device(): centre = lax.psum(picked, ('blk', 'grp')) / members]
where the time goes in v2:
time: 152 us; the launch traced here: 151 us
  blocking collectives  104 us (68%)
  between operations  14.2 us (9%)
  other arithmetic  8.71 us (6%)
  local copies, waits for them, and re-layouts  6.86 us (5%)
  matrix products  6.7 us (4%)
  waiting for transfers between devices  6.45 us (4%)
  starting transfers between devices  3.32 us (2%)
    all_gather x1, blocking collectives, summed_here(): parts = lax.all_gather(x, axis)  70.3 us
    all_gather x2, blocking collectives, joined_2(): everything = jax.tree.map(lambda part: lax.all_gather(part, axis), shard)  17.2 us
    all_gather x1, blocking collectives, per_device(): gathered = lax.all_gather(samples, 'grp', axis=1, tiled=True)  16.1 us
    all_to_all x1, waiting for transfers between devices, per_device(): lax.all_to_all(split_view, 'grp', split_axis=2, concat_axis=2, tiled=True)  5.73 us
    dot_general x1, matrix products, compute(): jnp.einsum('qd,kd->qk', queries, key_rows, precision=lax.Precision.HIGHEST)  5.35 us
    div x2, local copies, waits for them, and re-layouts, compute(): -distance / (2.0 * band_sq)  3.84 us
    all_to_all x1, starting transfers between devices, per_device(): lax.all_to_all(split_view, 'grp', split_axis=2, concat_axis=2, tiled=True)  3.32 us
  transfers between devices with their start and end apart: 2, of which 1 were waited for; matrix products, arithmetic and copies ran while one was open for 3% of the time, Pallas kernels for 0%

profile of v2, /device:TPU:0, one launch (start us, length us, event | category | flops | bytes accessed | tf_op | source)
XLA Modules:
  0.0 151.2 jit_solution(4682284197212759445)
XLA Ops:
  6.5 0.7 all-gather.8.cloned.1.call-update
  7.3 0.8 convert_reduce_fusion
  8.0 0.6 compare_reduce_fusion
  9.3 0.7 broadcast_subtract_fusion
  10.1 1.2 convolution_bitcast_fusion
  11.3 70.3 %all-gather.3 = f32[32,2,256]{2,1,0:T(2,128)S(1)} all-gather(f32[1,2,256]{2,1,0:T(2,128)S(1)} %convolution_bitcast_fusion), channel_id=2, replica_groups=mesh['blk'=8,'grp'=4] {'blk','grp'}, dimensions={0}, use_global_device_ids=true | all-gather | bytes 67584 | tf_op jit(solution)/shard_map/all_gather | solution.py:10
  81.6 16.1 %all_gather.24 = f32[4,128,256]{2,1,0:T(8,128)S(1)} all-gather(f32[4,32,256]{2,1,0:T(8,128)} %param.8), channel_id=1, replica_groups=mesh['blk'=8,'grp'=4] {'grp'}, dimensions={1}, use_global_device_ids=true | all-gather | bytes 655360 | tf_op jit(solution)/shard_map/all_gather | solution.py:69
  97.7 0.7 multiply_add_fusion
  98.4 14.7 %conditional.1 = (f32[2,512,32]{1,2,0:T(8,128)S(1)}) conditional(s32[]{:T(128)} %convert_element_type.15, () %tuple.36, (f32[4,128,256]{2,1,0:T(8,128)S(1)}, f32[32,32,256]{2,1,0:T(8,128)}, f32[2]{0:T(128)S(1)}) %tuple.37), branch_computations={%region_2.0_spmd, %region_3.10_spmd} | conditional | flops 1617689088 | bytes 25186376 | solution.py:46
  98.4 1.4 multiply_reduce_fusion
  99.9 0.7 fusion.12
  102.1 5.3 %broadcast_divide_fusion.1 = (f32[512,1024]{1,0:T(8,128)}, f32[512,1024]{1,0:T(8,128)}) fusion(f32[]{:T(128)} %bitcast.3, f32[]{:T(128)} %bitcast.6, f32[512,256]{1,0:T(8,128)S(1)} %bitcast.72, f32[1024,256]{1,0:T(8,128)} %bitcast.75, f32[1024]{0:T(1024)S(1)} %add.85, f32[512]{0:T(512)S(1)} %bitcast.81), kind=kOutput, calls=%fused_computation.10 | convolution fusion | flops 1613758464 | bytes 5773320 | tf_op jit(solution)/shard_map/cond/branch_1_fun/qd,kd->qk/dot_general | solution.py:33
  107.4 1.9 %copy.16 = f32[512,1024]{0,1:T(8,128)S(1)} copy(f32[512,1024]{1,0:T(8,128)} %get-tuple-element.190) | data formatting | bytes 4194304 | tf_op jit(solution)/shard_map/cond/branch_1_fun/div | solution.py:37
  109.7 0.5 fusion.3
  110.2 1.9 %copy.17 = f32[512,1024]{0,1:T(8,128)S(1)} copy(f32[512,1024]{1,0:T(8,128)} %get-tuple-element.191) | data formatting | bytes 4194304 | tf_op jit(solution)/shard_map/cond/branch_1_fun/div | solution.py:37
  112.5 0.5 fusion.1
  113.5 1.0 reshape.103
  114.5 3.3 %all-to-all-start = ((f32[4,1,8192]{2,1,0:T(1,128)}), f32[4,1,8192]{2,1,0:T(1,128)S(1)}, u32[]{:S(2)}, u32[]{:S(2)}) async-start(f32[4,1,8192]{2,1,0:T(1,128)} %reshape.103), calls=%async_computation | async-start | bytes 262144 | tf_op jit(solution)/shard_map/all_to_all | solution.py:79
  118.0 5.7 %all-to-all-done = f32[4,1,8192]{2,1,0:T(1,128)S(1)} async-done(((f32[4,1,8192]{2,1,0:T(1,128)}), f32[4,1,8192]{2,1,0:T(1,128)S(1)}, u32[]{:S(2)}, u32[]{:S(2)}) %all-to-all-start) | async-done | bytes 131104 | tf_op jit(solution)/shard_map/all_to_all | solution.py:79
  123.7 0.5 broadcast.47
  124.2 1.0 reduce.6
  126.4 9.0 %all-gather.5 = f32[4,2,4]{2,1,0:T(2,128)S(1)} all-gather(f32[1,2,4]{2,1,0:T(2,128)S(1)} %bitcast.80), channel_id=4, replica_groups=mesh['blk'=8,'grp'=4] {'grp'}, dimensions={0}, use_global_device_ids=true | all-gather | bytes 160 | tf_op jit(solution)/shard_map/all_gather | solution.py:15
  135.4 8.2 %all-gather.4 = f32[4,2,4]{2,1,0:T(2,128)S(1)} all-gather(f32[1,2,4]{2,1,0:T(2,128)S(1)} %bitcast.78), channel_id=3, replica_groups=mesh['blk'=8,'grp'=4] {'grp'}, dimensions={0}, use_global_device_ids=true | all-gather | bytes 160 | tf_op jit(solution)/shard_map/all_gather | solution.py:15
  143.7 0.7 subtract_subtract_fusion
  (32 shorter events, 3.0 us)
Async XLA Ops:
  6.5 91.9 %all-gather.8.cloned.1.call-start = ((), (), s32[]{:S(2)}) async-start(), calls=%async_computation.1 | async-start | bytes 1179648 | tf_op jit(solution)/shard_map/all_gather | solution.py:76
  113.1 4.8 %copy-start = (f32[4,32,256]{2,1,0:T(8,128)S(1)}, f32[4,32,256]{2,1,0:T(8,128)}, u32[]{:S(2)}) copy-start(f32[4,32,256]{2,1,0:T(8,128)} %param.8) | copy-start | bytes 393220
  114.5 9.2 %all-to-all-start = ((f32[4,1,8192]{2,1,0:T(1,128)}), f32[4,1,8192]{2,1,0:T(1,128)S(1)}, u32[]{:S(2)}, u32[]{:S(2)}) async-start(f32[4,1,8192]{2,1,0:T(1,128)} %reshape.103), calls=%async_computation | async-start | bytes 262144 | tf_op jit(solution)/shard_map/all_to_all | solution.py:79
Sparse Core Ops, SparseCore 0:
  9.2 26.1 all-gather.7
